TPU v7x, 512 devices: a 4x2x32 block of a 4x8x32 slice. The times are simulated.
512 devices in a mesh: shift: 2 (over y), blk: 128 (over z, x), depth: 2 (over core).
Axes of the slice: x: 4, y: 2, z: 32, core: 2. Of those that a mesh axis runs over, the one named last changes fastest.
The devices are a block of a 4x8x32 slice.
Arguments:
- density: bfloat16 [512, 32, 128, 128], P(('shift', 'blk')), parts along dimension 0, may hold values from -1.1953125 to 1.1953125
- product_tasks: int32 [3, 256, 4, 128], P(None, ('shift', 'blk')), parts along dimension 1, may hold values from 0 to 64, as said below
Outputs:
- square_blocks: bfloat16 [512, 32, 128, 128], P(('shift', 'blk'), 'depth'), parts along dimension 0
There are 2 independent parts, one for each index of `shift`. A program takes and returns all parts, laid end to end along the dimension named above; each array names one. Nothing has to cross between parts.
Inputs may be any that keep to these rules, and one draw needn't show every extreme that they name: `product_tasks`: for each panel r and offset t the first tasks are exactly the triples in which slot a of panel r holds block (i, j) of P with block row j in panel (r + t) mod 128, slot b of that panel holds block (j, k), and c is the slot of block (i, k) in block row i, where P's block pattern stores 32 distinct block columns in each block row, its own among them; each triple once; the rest are (0, 0, 64). Some panel and offset has exactly 128 triples.
All inputs are finite; a program needn't handle non-finite values.
Results may differ from a plain program's by a relative error of at most 0.001.
Values may be sent and summed in bfloat16 or wider, within the bound.
No kernel may reach another device: no remote copies, remote signals or barrier semaphores. Data moves between devices by JAX's collectives and lax.ppermute only.
A program may use at most 64 MiB of HBM per device.

v0:
```python
import jax
import jax.numpy as jnp
from jax import lax
from jax.sharding import PartitionSpec as P


def shifted(block, axis, distance):
    devices = range(lax.axis_size(axis))
    route = [((i - distance) % len(devices), i) for i in devices]
    return lax.ppermute(block, axis, route)


def split_up(value, dim, length):
    shape = value.shape
    tiles = value.reshape(*shape[:dim], length, shape[dim] // length, *shape[dim + 1 :])
    return jnp.moveaxis(tiles, dim, 0)


def summed_on_arrival(value, axis, dim):
    length = lax.axis_size(axis)
    tiles = lax.all_to_all(split_up(value, dim, length), axis, 0, 0, tiled=True)
    return jnp.sum(tiles, axis=0)


def multiply_step(total, mine, panel, tasks_now):
    count = tasks_now.shape[1]
    groups = 2
    grouped = tasks_now.reshape(3, groups, count // groups).transpose(1, 0, 2)
    segments = total.shape[0]

    def add_group(running, piece):
        first = jnp.take(mine, piece[0], axis=0)
        second = jnp.take(panel, piece[1], axis=0)
        products = jnp.einsum("nij,njk->nik", first, second, preferred_element_type=jnp.float32)
        return (running + jax.ops.segment_sum(products, piece[2], num_segments=segments), None)

    total, _ = lax.scan(add_group, total, grouped)
    return total


def body(density, product_tasks):
    rows, slots, size = (density.shape[0], density.shape[1], density.shape[2])
    mine = density.reshape(rows * slots, size, size)
    tasks_here = product_tasks[:, 0]
    window = tasks_here.shape[1]
    layers = lax.axis_size("depth")
    steps = window // layers
    layer = lax.axis_index("depth")
    total = jnp.zeros((rows * slots + 1, size, size), jnp.float32)
    distant = shifted(mine, "blk", -steps)
    panel = jnp.where(layer == 0, mine, distant)
    for step in range(steps):
        if step > 0:
            panel = shifted(panel, "blk", -1)
        offset = layer * steps + step
        tasks_now = lax.dynamic_index_in_dim(tasks_here, offset, 1, keepdims=False)
        total = multiply_step(total, mine, panel, tasks_now)
    partial_value = total[: rows * slots].reshape(rows, slots, size, size)
    summed = summed_on_arrival(partial_value, "depth", 1)
    return summed.astype(jnp.bfloat16)


def solution(mesh):
    placed = (P(("shift", "blk"), None, None, None), P(None, ("shift", "blk"), None, None))
    return jax.shard_map(
        body,
        mesh=mesh,
        in_specs=placed,
        out_specs=P(("shift", "blk"), "depth", None, None),
        check_vma=False,
    )
```

profile of v0, /device:TPU:33, one launch (start us, length us, event | category | flops | bytes accessed | tf_op | source)
XLA Modules:
  0.0 221.3 jit_solution(4289043629335712524)
XLA Ops:
  0.0 48.6 %collective-permute-start = (bf16[64,128,128]{2,1,0:T(8,128)(2,1)}, bf16[64,128,128]{2,1,0:T(8,128)(2,1)S(1)}, u32[]{:S(2)}, u32[]{:S(2)}) collective-permute-start(bf16[64,128,128]{2,1,0:T(8,128)(2,1)} %bitcast.47), channel_id=1, source_target_pairs={{4,0},{6,2},{8,4},{10,6},{12,8},{14,10},{16,12},{18,14},{20,16},{2... | collective-permute-start | bytes 6291464 | tf_op jit(solution)/shard_map/ppermute | solution.py:10
  48.6 0.0 copy-start.1
  48.6 44.7 %collective-permute-done = bf16[64,128,128]{2,1,0:T(8,128)(2,1)S(1)} collective-permute-done((bf16[64,128,128]{2,1,0:T(8,128)(2,1)}, bf16[64,128,128]{2,1,0:T(8,128)(2,1)S(1)}, u32[]{:S(2)}, u32[]{:S(2)}) %collective-permute-start) | collective-permute-done | bytes 2097184 | tf_op jit(solution)/shard_map/ppermute | solution.py:10
  93.3 3.1 %broadcast_select_fusion = bf16[64,128,128]{2,1,0:T(8,128)(2,1)} fusion(bf16[64,128,128]{2,1,0:T(8,128)(2,1)S(1)} %collective-permute-done, pred[]{:T(512)S(6)} %eq.3, bf16[2,32,128,128]{3,2,1,0:T(8,128)(2,1)} %param.8), kind=kLoop, calls=%fused_computation.44 | loop fusion | flops 1048576 | bytes 6291457 | tf_op jit(solution)/shard_map/jit(_where)/select_n | solution.py:51
  96.4 7.5 %collective-permute-start.1 = (bf16[64,128,128]{2,1,0:T(8,128)(2,1)}, bf16[64,128,128]{2,1,0:T(8,128)(2,1)}, u32[]{:S(2)}, u32[]{:S(2)}) collective-permute-start(bf16[64,128,128]{2,1,0:T(8,128)(2,1)} %broadcast_select_fusion), channel_id=1, source_target_pairs={{2,0},{4,2},{6,4},{8,6},{10,8},{12,10},{14,12},{16,14},{18,16},{20... | collective-permute-start | bytes 6291464 | tf_op jit(solution)/shard_map/ppermute | solution.py:10
  103.9 0.0 copy-done.1
  104.0 0.1 reshape.32
  104.0 0.1 reshape.34
  104.1 0.0 copy-start
  104.1 2.5 %broadcast.8 = f32[65,128,128]{2,1,0:T(8,128)} broadcast(f32[]{:T(128)} %constant.35.clone.1), dimensions={} | broadcast | bytes 4259844 | tf_op jit(solution)/shard_map/broadcast.5
  106.6 0.0 copy-done
  106.6 49.7 %while.20 = (s32[]{:T(128)}, f32[65,128,128]{2,1,0:T(8,128)}, s32[2,3,64]{2,0,1:T(2,128)S(1)}, bf16[64,128,128]{2,1,0:T(8,128)(2,1)S(1)}, bf16[64,128,128]{2,1,0...) while((s32[]{:T(128)}, f32[65,128,128]{2,1,0:T(8,128)}, s32[2,3,64]{2,0,1:T(2,128)S(1)}, ...), condition=%wide.region_2.4_spmd, body=%wide.region_0.3_spmd.sunk | while | flops 271584000 | bytes 29371524 | solution.py:37
  106.6 3.7 %gather_fusion = bf16[64,128,128]{2,1,0:T(8,128)(2,1)} fusion(bf16[64,128,128]{2,1,0:T(8,128)(2,1)} %get-tuple-element.238, s32[1024]{0:T(1024)S(1)} %get-tuple-element.201), kind=kCustom, calls=%fused_computation.1.clone.clone.1 | custom fusion | bytes 4194560 | tf_op jit(solution)/shard_map/while/body/eval_jaxpr/jit(_take)/gather | solution.py:33
  110.4 2.1 gather_fusion.1
  112.5 5.0 %fusion.31 = f32[64,128,128]{2,1,0:T(8,128)} fusion(bf16[64,128,128]{2,1,0:T(8,128)(2,1)} %gather_fusion, bf16[64,128,128]{2,1,0:T(8,128)(2,1)} %gather_fusion.1, pred[64]{0:T(512)(128)(4,1)S(1)} %get-tuple-element.203, pred[64]{0:T(512)(128)(4,1)S(1)} %get-tuple-element.204), kind=kOutput, calls=%fused_computation.6.clone.1 | convolution fusion | flops 270532608 | bytes 8388736 | tf_op jit(solution)/shard_map/while/body/eval_jaxpr/nij,njk->nik/dot_general | solution.py:34
  117.5 13.7 %scatter_fusion = f32[65,128,128]{2,1,0:T(8,128)} fusion(f32[65,128,128]{2,1,0:T(8,128)} %get-tuple-element.226, s32[64]{0:T(128)S(1)} %fusion.30, f32[64,128,128]{2,1,0:T(8,128)} %fusion.31), kind=kCustom, calls=%fused_computation.4.clone.1 | custom fusion | flops 1048576 | bytes 12583168 | tf_op jit(solution)/shard_map/while/body/eval_jaxpr/scatter-add | solution.py:35
  131.2 3.7 %gather_fusion = bf16[64,128,128]{2,1,0:T(8,128)(2,1)} fusion(bf16[64,128,128]{2,1,0:T(8,128)(2,1)} %get-tuple-element.238, s32[1024]{0:T(1024)S(1)} %get-tuple-element.201), kind=kCustom, calls=%fused_computation.1.clone.clone.1 | custom fusion | bytes 4194560 | tf_op jit(solution)/shard_map/while/body/eval_jaxpr/jit(_take)/gather | solution.py:33
  134.9 2.1 gather_fusion.1
  137.1 5.0 %fusion.31 = f32[64,128,128]{2,1,0:T(8,128)} fusion(bf16[64,128,128]{2,1,0:T(8,128)(2,1)} %gather_fusion, bf16[64,128,128]{2,1,0:T(8,128)(2,1)} %gather_fusion.1, pred[64]{0:T(512)(128)(4,1)S(1)} %get-tuple-element.203, pred[64]{0:T(512)(128)(4,1)S(1)} %get-tuple-element.204), kind=kOutput, calls=%fused_computation.6.clone.1 | convolution fusion | flops 270532608 | bytes 8388736 | tf_op jit(solution)/shard_map/while/body/eval_jaxpr/nij,njk->nik/dot_general | solution.py:34
  142.1 14.2 %scatter_fusion = f32[65,128,128]{2,1,0:T(8,128)} fusion(f32[65,128,128]{2,1,0:T(8,128)} %get-tuple-element.226, s32[64]{0:T(128)S(1)} %fusion.30, f32[64,128,128]{2,1,0:T(8,128)} %fusion.31), kind=kCustom, calls=%fused_computation.4.clone.1 | custom fusion | flops 1048576 | bytes 12583168 | tf_op jit(solution)/shard_map/while/body/eval_jaxpr/scatter-add | solution.py:35
  156.3 0.0 collective-permute-done.1
  156.3 49.8 %while.21 = (s32[]{:T(128)}, f32[65,128,128]{2,1,0:T(8,128)}, s32[2,3,64]{2,0,1:T(2,128)S(1)}, bf16[64,128,128]{2,1,0:T(8,128)(2,1)S(1)}, bf16[64,128,128]{2,1,0...) while((s32[]{:T(128)}, f32[65,128,128]{2,1,0:T(8,128)}, s32[2,3,64]{2,0,1:T(2,128)S(1)}, ...), condition=%wide.region_5.7_spmd, body=%wide.region_3.6_spmd.sunk | while | flops 271584000 | bytes 29371524 | solution.py:37
  156.3 3.7 %gather_fusion.2 = bf16[64,128,128]{2,1,0:T(8,128)(2,1)} fusion(bf16[64,128,128]{2,1,0:T(8,128)(2,1)} %get-tuple-element.265, s32[1024]{0:T(1024)S(1)} %get-tuple-element.212), kind=kCustom, calls=%fused_computation.3.clone.clone.1 | custom fusion | bytes 4194560 | tf_op jit(solution)/shard_map/while/body/eval_jaxpr/jit(_take)/gather | solution.py:33
  160.1 2.1 gather_fusion.3
  162.2 5.0 %fusion.35 = f32[64,128,128]{2,1,0:T(8,128)} fusion(bf16[64,128,128]{2,1,0:T(8,128)(2,1)} %gather_fusion.2, bf16[64,128,128]{2,1,0:T(8,128)(2,1)} %gather_fusion.3, pred[64]{0:T(512)(128)(4,1)S(1)} %get-tuple-element.214, pred[64]{0:T(512)(128)(4,1)S(1)} %get-tuple-element.215), kind=kOutput, calls=%fused_computation.25.clone.1 | convolution fusion | flops 270532608 | bytes 8388736 | tf_op jit(solution)/shard_map/while/body/eval_jaxpr/nij,njk->nik/dot_general | solution.py:34
  167.2 13.7 %scatter_fusion.1 = f32[65,128,128]{2,1,0:T(8,128)} fusion(f32[65,128,128]{2,1,0:T(8,128)} %get-tuple-element.253, s32[64]{0:T(128)S(1)} %fusion.34, f32[64,128,128]{2,1,0:T(8,128)} %fusion.35), kind=kCustom, calls=%fused_computation.5.clone.1 | custom fusion | flops 1048576 | bytes 12583168 | tf_op jit(solution)/shard_map/while/body/eval_jaxpr/scatter-add | solution.py:35
  180.9 3.7 %gather_fusion.2 = bf16[64,128,128]{2,1,0:T(8,128)(2,1)} fusion(bf16[64,128,128]{2,1,0:T(8,128)(2,1)} %get-tuple-element.265, s32[1024]{0:T(1024)S(1)} %get-tuple-element.212), kind=kCustom, calls=%fused_computation.3.clone.clone.1 | custom fusion | bytes 4194560 | tf_op jit(solution)/shard_map/while/body/eval_jaxpr/jit(_take)/gather | solution.py:33
  184.6 2.1 gather_fusion.3
  186.8 5.0 %fusion.35 = f32[64,128,128]{2,1,0:T(8,128)} fusion(bf16[64,128,128]{2,1,0:T(8,128)(2,1)} %gather_fusion.2, bf16[64,128,128]{2,1,0:T(8,128)(2,1)} %gather_fusion.3, pred[64]{0:T(512)(128)(4,1)S(1)} %get-tuple-element.214, pred[64]{0:T(512)(128)(4,1)S(1)} %get-tuple-element.215), kind=kOutput, calls=%fused_computation.25.clone.1 | convolution fusion | flops 270532608 | bytes 8388736 | tf_op jit(solution)/shard_map/while/body/eval_jaxpr/nij,njk->nik/dot_general | solution.py:34
  191.8 14.4 %scatter_fusion.1 = f32[65,128,128]{2,1,0:T(8,128)} fusion(f32[65,128,128]{2,1,0:T(8,128)} %get-tuple-element.253, s32[64]{0:T(128)S(1)} %fusion.34, f32[64,128,128]{2,1,0:T(8,128)} %fusion.35), kind=kCustom, calls=%fused_computation.5.clone.1 | custom fusion | flops 1048576 | bytes 12583168 | tf_op jit(solution)/shard_map/while/body/eval_jaxpr/scatter-add | solution.py:35
  206.1 2.5 %slice.27 = f32[64,128,128]{2,1,0:T(8,128)S(1)} slice(f32[65,128,128]{2,1,0:T(8,128)} %get-tuple-element.61), slice={[0:64], [0:128], [0:128]} | slice | bytes 8388608 | tf_op jit(solution)/shard_map/slice | solution.py:58
  208.6 0.5 copy.9
  209.1 8.5 %all_to_all.5 = f32[2,2,16,128,128]{4,3,2,1,0:T(8,128)} all-to-all(f32[2,2,16,128,128]{4,3,2,1,0:T(8,128)S(1)} %copy.9), channel_id=1, replica_groups=mesh['shift'=2,'blk'=128,'depth'=2] {'depth'}, dimensions={0} | all-to-all | bytes 8388608 | tf_op jit(solution)/shard_map/all_to_all | solution.py:21
  217.5 3.8 %reduce_sum.9 = bf16[2,16,128,128]{3,2,1,0:T(8,128)(2,1)} reduce(f32[2,2,16,128,128]{4,3,2,1,0:T(8,128)} %all_to_all.5, f32[]{:T(128)} %constant.35.clone.1), dimensions={0}, to_apply=%region_6.8 | reduce | flops 524288 | bytes 5242884 | tf_op jit(solution)/shard_map/reduce_sum | solution.py:22
  (13 shorter events, 0.1 us)
Async XLA Ops:
  0.0 93.3 %collective-permute-start = (bf16[64,128,128]{2,1,0:T(8,128)(2,1)}, bf16[64,128,128]{2,1,0:T(8,128)(2,1)S(1)}, u32[]{:S(2)}, u32[]{:S(2)}) collective-permute-start(bf16[64,128,128]{2,1,0:T(8,128)(2,1)} %bitcast.47), channel_id=1, source_target_pairs={{4,0},{6,2},{8,4},{10,6},{12,8},{14,10},{16,12},{18,14},{20,16},{2... | collective-permute-start | bytes 6291464 | tf_op jit(solution)/shard_map/ppermute | solution.py:10
  48.6 55.3 %copy-start.1 = (s32[3,1,4,128]{3,2,1,0:T(4,128)S(1)}, s32[3,1,4,128]{3,2,1,0:T(4,128)}, u32[]{:S(2)}) copy-start(s32[3,1,4,128]{3,2,1,0:T(4,128)} %param.9) | copy-start | bytes 18436
  96.4 59.9 %collective-permute-start.1 = (bf16[64,128,128]{2,1,0:T(8,128)(2,1)}, bf16[64,128,128]{2,1,0:T(8,128)(2,1)}, u32[]{:S(2)}, u32[]{:S(2)}) collective-permute-start(bf16[64,128,128]{2,1,0:T(8,128)(2,1)} %broadcast_select_fusion), channel_id=1, source_target_pairs={{2,0},{4,2},{6,4},{8,6},{10,8},{12,10},{14,12},{16,14},{18,16},{20... | collective-permute-start | bytes 6291464 | tf_op jit(solution)/shard_map/ppermute | solution.py:10
  104.1 2.5 %copy-start = (bf16[2,32,128,128]{3,2,1,0:T(8,128)(2,1)S(1)}, bf16[2,32,128,128]{3,2,1,0:T(8,128)(2,1)}, u32[]{:S(2)}) copy-start(bf16[2,32,128,128]{3,2,1,0:T(8,128)(2,1)} %param.8) | copy-start | bytes 6291460
where the time goes:
time: 222 us; the launch traced here: 221 us
  other arithmetic  62.9 us (28%)
  starting transfers between devices  56.1 us (25%)
  waiting for transfers between devices  44.7 us (20%)
  local copies, waits for them, and re-layouts  29.1 us (13%)
  matrix products  20 us (9%)
  blocking collectives  8.46 us (4%)
    ppermute x2, starting transfers between devices, shifted(): return lax.ppermute(block, axis, route)  56.1 us
    scatter-add x4, other arithmetic, add_group(): jax.ops.segment_sum(products, piece[2], num_segments=segments)  56 us
    ppermute x2, waiting for transfers between devices, shifted(): return lax.ppermute(block, axis, route)  44.7 us
    dot_general x4, matrix products, add_group(): jnp.einsum('nij,njk->nik', first, second, preferred_element_type=jnp.floa...  20 us
    gather x4, local copies, waits for them, and re-layouts, add_group(): second = jnp.take(panel, piece[1], axis=0)  14.9 us
    gather x4, local copies, waits for them, and re-layouts, add_group(): first = jnp.take(mine, piece[0], axis=0)  8.53 us
    all_to_all x1, blocking collectives, summed_on_arrival(): tiles = lax.all_to_all(split_up(value, dim, length), axis, 0, 0, tiled=True)  8.46 us
  transfers between devices with their start and end apart: 2, of which 1 were waited for; matrix products, arithmetic and copies ran while one was open for 24% of the time, Pallas kernels for 0%

commit v1 on v0

v1 whole, which is shorter than its diff:
```python
import functools

import jax
import jax.numpy as jnp
from jax import lax
from jax.experimental import pallas as pl
from jax.experimental.pallas import tpu as pltpu
from jax.sharding import PartitionSpec as P


UNROLL = 8
SENDER = 0
WORKER = 1


def move(value, routes):
    layers = lax.axis_size("depth")
    pairs = [(a * layers + b, c * layers + d) for (a, b), (c, d) in routes]
    return lax.ppermute(value, ("blk", "depth"), pairs)


def run_tasks(tasks, offset, groups, mine, panel, total):
    def group(step, carry):
        base = step * UNROLL
        products = []
        for n in range(UNROLL):
            first = mine[tasks[0, offset, base + n]]
            second = panel[tasks[1, offset, base + n]]
            products.append(jnp.dot(first, second, preferred_element_type=jnp.float32))
        for n in range(UNROLL):
            slot = tasks[2, offset, base + n]
            total[slot] = total[slot] + products[n]
        return carry

    lax.fori_loop(0, groups, group, 0)


def begin_kernel(counts, tasks, mine, total):
    def clear(slot, carry):
        total[slot] = jnp.zeros(total.shape[1:], total.dtype)
        return carry

    lax.fori_loop(0, total.shape[0], clear, 0)
    run_tasks(tasks, 0, counts[0], mine, mine, total)


def middle_kernel(offsets, counts, tasks, mine, *refs):
    panels, total = refs[: len(offsets)], refs[-1]
    for place, (offset, panel) in enumerate(zip(offsets, panels)):
        run_tasks(tasks, offset, counts[place], mine, panel, total)


def last_kernel(offsets, counts, tasks, mine, *refs):
    panels, total = refs[: len(offsets)], refs[len(offsets)]
    low, high = refs[-2:]
    for place, (offset, panel) in enumerate(zip(offsets, panels)):
        run_tasks(tasks, offset, counts[place], mine, panel, total)
    rows, half = low.shape[0], low.shape[1]

    @pl.when(counts[len(offsets)] > 0)
    def _():
        for row in range(rows):

            def put(slot, carry):
                low[row, slot] = total[row * 2 * half + slot].astype(low.dtype)
                high[row, slot] = total[row * 2 * half + half + slot].astype(high.dtype)
                return carry

            lax.fori_loop(0, half, put, 0)


SMEM = functools.partial(pl.BlockSpec, memory_space=pltpu.SMEM)
VMEM = functools.partial(pl.BlockSpec, memory_space=pltpu.VMEM)

PARAMS = pltpu.CompilerParams(vmem_limit_bytes=24 * 1024 * 1024)


def cost(blocks, size, tasks):
    return pl.CostEstimate(
        flops=2 * tasks * size**3, bytes_accessed=blocks * size * size * 2, transcendentals=0
    )


def body(density, product_tasks):
    rows, slots, size = density.shape[0], density.shape[1], density.shape[2]
    mine = density.reshape(rows * slots, size, size)
    tasks = product_tasks[:, 0]
    window, places = tasks.shape[1], tasks.shape[2]
    count = lax.axis_size("blk")
    lines = range(count // window)

    def at(line, column):
        return line % len(lines) * window + column

    inner = range(1, window)
    near = [((at(z, x), WORKER), (at(z, x - 1), WORKER)) for z in lines for x in inner]
    far = [((at(z, window - 1), WORKER), (at(z, 0), WORKER)) for z in lines]
    far += [((at(z + 1, x - 1), SENDER), (at(z, x), WORKER)) for z in lines for x in inner]
    ahead = [((at(z, 0), WORKER), (at(z, window - 1), SENDER)) for z in lines]
    across = [((at(z + 1, window - 1), SENDER), (at(z, window - 1), WORKER)) for z in lines]
    up = [((at(z, x - 1), WORKER), (at(z, x), WORKER)) for z in lines for x in inner]
    down = [((at(z, 1), WORKER), (at(z, 0), WORKER)) for z in lines]
    halves = [((p, WORKER), (p, SENDER)) for p in range(count)]

    column = lax.axis_index("blk") % window
    works = lax.axis_index("depth") == WORKER
    groups = jnp.where(works, places // UNROLL, 0).astype(jnp.int32)
    first, final = column == 0, column == window - 1

    moved = move(mine, ahead)
    one = move(mine, near)
    three = move(mine, far)
    crossed = move(moved, across)
    two_up = move(three, up)
    two_down = move(one, down)

    sums = jax.ShapeDtypeStruct((rows * slots + 1, size, size), jnp.float32)
    total = pl.pallas_call(
        begin_kernel,
        out_shape=sums,
        in_specs=[SMEM(), SMEM(), VMEM()],
        out_specs=VMEM(),
        cost_estimate=cost(slots, size, places),
        compiler_params=PARAMS,
        name="begin",
    )(jnp.stack([groups]), tasks, mine)
    counts = jnp.stack([jnp.where(final, 0, groups), groups])
    total = pl.pallas_call(
        functools.partial(middle_kernel, (1, 3)),
        out_shape=sums,
        in_specs=[SMEM(), SMEM(), VMEM(), VMEM(), VMEM(), VMEM()],
        out_specs=VMEM(),
        input_output_aliases={5: 0},
        cost_estimate=cost(slots, size, 2 * places),
        compiler_params=PARAMS,
        name="middle",
    )(counts, tasks, mine, one, three, total)
    counts = jnp.stack(
        [jnp.where(first, 0, groups), jnp.where(first, groups, 0), jnp.where(final, groups, 0), groups]
    )
    half = jax.ShapeDtypeStruct((rows, slots // 2, size, size), jnp.bfloat16)
    low, high = pl.pallas_call(
        functools.partial(last_kernel, (2, 2, 1)),
        out_shape=(half, half),
        in_specs=[SMEM(), SMEM(), VMEM(), VMEM(), VMEM(), VMEM(), VMEM()],
        out_specs=(VMEM(), VMEM()),
        cost_estimate=cost(slots, size, places),
        compiler_params=PARAMS,
        name="last",
    )(counts, tasks, mine, two_up, two_down, crossed, total)
    arrived = move(low, halves)
    return jnp.where(works, high, arrived)


def solution(mesh):
    placed = (P(("shift", "blk"), None, None, None), P(None, ("shift", "blk"), None, None))
    return jax.shard_map(
        body,
        mesh=mesh,
        in_specs=placed,
        out_specs=P(("shift", "blk"), "depth", None, None),
        check_vma=False,
    )
```

time: 222 us -> 110 us (0.50)
  the two profiles are of different devices: /device:TPU:33 before, /device:TPU:39 now
where the time goes in v1:
time: 110 us
  starting transfers between devices  47 us (43%)
  waiting for transfers between devices  38.6 us (35%)
  Pallas kernels  20.7 us (19%)
  local copies, waits for them, and re-layouts  2.28 us (2%)
  other arithmetic  1.24 us (1%)
    ppermute x7, starting transfers between devices, move(): return lax.ppermute(value, ('blk', 'depth'), pairs)  47 us
    ppermute x7, waiting for transfers between devices, move(): return lax.ppermute(value, ('blk', 'depth'), pairs)  38.6 us
    pallas_call x1, Pallas kernels, body(): pl.pallas_call(functools.partial(last_kernel, (2, 2, 1)), out_shape=(half...  10 us
    pallas_call x1, Pallas kernels, body(): pl.pallas_call(functools.partial(middle_kernel, (1, 3)), out_shape=sums,...  6.01 us
    pallas_call x1, Pallas kernels, body(): pl.pallas_call(begin_kernel, out_shape=sums, in_specs=[SMEM(), SMEM(), VM...  4.67 us
    unnamed x4, local copies, waits for them, and re-layouts  2.28 us
  transfers between devices with their start and end apart: 7, of which 4 were waited for; matrix products, arithmetic and copies ran while one was open for 0% of the time, Pallas kernels for 10%

profile of v1, /device:TPU:39, one launch (start us, length us, event | category | flops | bytes accessed | tf_op | source)
XLA Modules:
  0.0 110.0 jit_solution(8246666936949872355)
XLA Ops:
  0.0 1.9 %collective-permute-start = (bf16[64,128,128]{2,1,0:T(8,128)(2,1)}, bf16[64,128,128]{2,1,0:T(8,128)(2,1)}, u32[]{:S(2)}, u32[]{:S(2)}) collective-permute-start(bf16[64,128,128]{2,1,0:T(8,128)(2,1)} %bitcast.7), channel_id=1, source_target_pairs={{7,1},{15,9},{23,17},{31,25},{39,33},{47,41},{55,49},{63,57},{71,6... | collective-permute-start | bytes 6291464 | tf_op jit(solution)/shard_map/ppermute | solution.py:19
  1.9 3.0 %collective-permute-start.2 = (bf16[64,128,128]{2,1,0:T(8,128)(2,1)}, bf16[64,128,128]{2,1,0:T(8,128)(2,1)}, u32[]{:S(2)}, u32[]{:S(2)}) collective-permute-start(bf16[64,128,128]{2,1,0:T(8,128)(2,1)} %bitcast.8), channel_id=1, source_target_pairs={{3,1},{5,3},{7,5},{11,9},{13,11},{15,13},{19,17},{21,19},{23,21},{... | collective-permute-start | bytes 6291464 | tf_op jit(solution)/shard_map/ppermute | solution.py:19
  5.0 2.0 %collective-permute-start.4 = (bf16[64,128,128]{2,1,0:T(8,128)(2,1)}, bf16[64,128,128]{2,1,0:T(8,128)(2,1)}, u32[]{:S(2)}, u32[]{:S(2)}) collective-permute-start(bf16[64,128,128]{2,1,0:T(8,128)(2,1)} %bitcast.9), channel_id=1, source_target_pairs={{1,6},{9,14},{17,22},{25,30},{33,38},{41,46},{49,54},{57,62},{65,7... | collective-permute-start | bytes 6291464 | tf_op jit(solution)/shard_map/ppermute | solution.py:19
  7.0 21.9 %collective-permute-done.refs_1_ = bf16[64,128,128]{2,1,0:T(8,128)(2,1)} collective-permute-done((bf16[64,128,128]{2,1,0:T(8,128)(2,1)}, bf16[64,128,128]{2,1,0:T(8,128)(2,1)}, u32[]{:S(2)}, u32[]{:S(2)}) %collective-permute-start) | collective-permute-done | bytes 2097184 | tf_op jit(solution)/shard_map/ppermute | solution.py:19
  28.9 1.3 %collective-permute-start.1 = (bf16[64,128,128]{2,1,0:T(8,128)(2,1)}, bf16[64,128,128]{2,1,0:T(8,128)(2,1)S(1)}, u32[]{:S(2)}, u32[]{:S(2)}) collective-permute-start(bf16[64,128,128]{2,1,0:T(8,128)(2,1)} %collective-permute-done.refs_1_), channel_id=1, source_target_pairs={{1,3},{3,5},{5,7},{9,11},{11,13},{13,15},{17,19},{19,21},{21,23},{... | collective-permute-start | bytes 6291464 | tf_op jit(solution)/shard_map/ppermute | solution.py:19
  30.2 0.0 collective-permute-done.2.refs_0_
  30.2 2.0 %collective-permute-start.3 = (bf16[64,128,128]{2,1,0:T(8,128)(2,1)}, bf16[64,128,128]{2,1,0:T(8,128)(2,1)}, u32[]{:S(2)}, u32[]{:S(2)}) collective-permute-start(bf16[64,128,128]{2,1,0:T(8,128)(2,1)} %collective-permute-done.2.refs_0_), channel_id=1, source_target_pairs={{3,1},{11,9},{19,17},{27,25},{35,33},{43,41},{51,49},{59,57},{67,6... | collective-permute-start | bytes 6291464 | tf_op jit(solution)/shard_map/ppermute | solution.py:19
  32.2 0.0 collective-permute-done.4
  32.2 1.3 %collective-permute-start.5 = (bf16[64,128,128]{2,1,0:T(8,128)(2,1)}, bf16[64,128,128]{2,1,0:T(8,128)(2,1)}, u32[]{:S(2)}, u32[]{:S(2)}) collective-permute-start(bf16[64,128,128]{2,1,0:T(8,128)(2,1)} %collective-permute-done.4), channel_id=1, source_target_pairs={{14,7},{22,15},{30,23},{38,31},{46,39},{54,47},{62,55},{70,63},{78... | collective-permute-start | bytes 6291464 | tf_op jit(solution)/shard_map/ppermute | solution.py:19
  33.5 0.0 copy-start
  33.5 1.6 %copy-done = bf16[2,32,128,128]{3,2,1,0:T(8,128)(2,1)S(1)} copy-done((bf16[2,32,128,128]{3,2,1,0:T(8,128)(2,1)S(1)}, bf16[2,32,128,128]{3,2,1,0:T(8,128)(2,1)}, u32[]{:S(2)}) %copy-start) | copy-done | bytes 2097176
  35.1 0.0 copy-start.1
  35.1 0.7 copy-done.1
  35.8 4.7 %begin.1.refs_2_ = f32[65,128,128]{2,1,0:T(8,128)S(1)} custom-call(s32[1]{0:T(128)} %bitcast.3.counts, s32[3,4,128]{2,1,0:T(4,128)S(1)} %bitcast.13, bf16[64,128,128]{2,1,0:T(8,128)(2,1)S(1)} %bitcast.10), custom_call_target="tpu_custom_call" | custom-call | flops 536870912 | bytes 1048576 | tf_op jit(solution)/shard_map/begin/pallas_call | solution.py:118
  40.5 0.1 pad_add_fusion.1.counts
  40.6 0.1 pad_add_fusion.counts
  40.6 6.0 %middle.1.refs_3_ = f32[65,128,128]{2,1,0:T(8,128)S(1)} custom-call(s32[2]{0:T(128)S(1)} %pad_add_fusion.1.counts, s32[3,4,128]{2,1,0:T(4,128)S(1)} %bitcast.14, bf16[64,128,128]{2,1,0:T(8,128)(2,1)S(1)} %bitcast.11, bf16[64,128,128]{2,1,0:T(8,128)(2,1)} %collective-permute-done.2.refs_0_, ...), custom_call_target="tpu_custom_call", output_to_operand_aliasing={{}: (5, {})} | custom-call | flops 1073741824 | bytes 1048576 | tf_op jit(solution)/shard_map/middle/pallas_call | solution.py:128
  46.7 9.2 %collective-permute-done.1.refs_0_ = bf16[64,128,128]{2,1,0:T(8,128)(2,1)S(1)} collective-permute-done((bf16[64,128,128]{2,1,0:T(8,128)(2,1)}, bf16[64,128,128]{2,1,0:T(8,128)(2,1)S(1)}, u32[]{:S(2)}, u32[]{:S(2)}) %collective-permute-start.1) | collective-permute-done | bytes 2097184 | tf_op jit(solution)/shard_map/ppermute | solution.py:19
  55.9 0.0 collective-permute-done.3.refs_1_
  55.9 5.3 %collective-permute-done.5.refs_2_ = bf16[64,128,128]{2,1,0:T(8,128)(2,1)} collective-permute-done((bf16[64,128,128]{2,1,0:T(8,128)(2,1)}, bf16[64,128,128]{2,1,0:T(8,128)(2,1)}, u32[]{:S(2)}, u32[]{:S(2)}) %collective-permute-start.5) | collective-permute-done | bytes 2097184 | tf_op jit(solution)/shard_map/ppermute | solution.py:19
  61.2 10.0 %last.1 = (bf16[2,16,128,128]{3,2,1,0:T(8,128)(2,1)S(1)}, bf16[2,16,128,128]{3,2,1,0:T(8,128)(2,1)S(1)}) custom-call(s32[4]{0:T(128)S(1)} %pad_add_fusion.counts, s32[3,4,128]{2,1,0:T(4,128)S(1)} %bitcast.15, bf16[64,128,128]{2,1,0:T(8,128)(2,1)S(1)} %bitcast.12, bf16[64,128,128]{2,1,0:T(8,128)(2,1)S(1)} %collective-permute-done.1.refs_0_, ...), custom_call_target="tpu_custom_call" | custom-call | flops 536870912 | bytes 1048576 | tf_op jit(solution)/shard_map/last/pallas_call | solution.py:142
  71.2 35.5 %collective-permute-start.6 = (bf16[2,16,128,128]{3,2,1,0:T(8,128)(2,1)S(1)}, bf16[2,16,128,128]{3,2,1,0:T(8,128)(2,1)S(1)}, u32[]{:S(2)}, u32[]{:S(2)}) collective-permute-start(bf16[2,16,128,128]{3,2,1,0:T(8,128)(2,1)S(1)} %get-tuple-element.8), channel_id=1, source_target_pairs={{1,0},{3,2},{5,4},{7,6},{9,8},{11,10},{13,12},{15,14},{17,16},{19,... | collective-permute-start | bytes 3145736 | tf_op jit(solution)/shard_map/ppermute | solution.py:19
  106.7 2.2 %collective-permute-done.6 = bf16[2,16,128,128]{3,2,1,0:T(8,128)(2,1)S(1)} collective-permute-done((bf16[2,16,128,128]{3,2,1,0:T(8,128)(2,1)S(1)}, bf16[2,16,128,128]{3,2,1,0:T(8,128)(2,1)S(1)}, u32[]{:S(2)}, u32[]{:S(2)}) %collective-permute-start.6) | collective-permute-done | bytes 1048608 | tf_op jit(solution)/shard_map/ppermute | solution.py:19
  108.9 1.1 broadcast_select_fusion
Async XLA Ops:
  0.0 28.9 %collective-permute-start = (bf16[64,128,128]{2,1,0:T(8,128)(2,1)}, bf16[64,128,128]{2,1,0:T(8,128)(2,1)}, u32[]{:S(2)}, u32[]{:S(2)}) collective-permute-start(bf16[64,128,128]{2,1,0:T(8,128)(2,1)} %bitcast.7), channel_id=1, source_target_pairs={{7,1},{15,9},{23,17},{31,25},{39,33},{47,41},{55,49},{63,57},{71,6... | collective-permute-start | bytes 6291464 | tf_op jit(solution)/shard_map/ppermute | solution.py:19
  1.9 28.2 %collective-permute-start.2 = (bf16[64,128,128]{2,1,0:T(8,128)(2,1)}, bf16[64,128,128]{2,1,0:T(8,128)(2,1)}, u32[]{:S(2)}, u32[]{:S(2)}) collective-permute-start(bf16[64,128,128]{2,1,0:T(8,128)(2,1)} %bitcast.8), channel_id=1, source_target_pairs={{3,1},{5,3},{7,5},{11,9},{13,11},{15,13},{19,17},{21,19},{23,21},{... | collective-permute-start | bytes 6291464 | tf_op jit(solution)/shard_map/ppermute | solution.py:19
  5.0 27.2 %collective-permute-start.4 = (bf16[64,128,128]{2,1,0:T(8,128)(2,1)}, bf16[64,128,128]{2,1,0:T(8,128)(2,1)}, u32[]{:S(2)}, u32[]{:S(2)}) collective-permute-start(bf16[64,128,128]{2,1,0:T(8,128)(2,1)} %bitcast.9), channel_id=1, source_target_pairs={{1,6},{9,14},{17,22},{25,30},{33,38},{41,46},{49,54},{57,62},{65,7... | collective-permute-start | bytes 6291464 | tf_op jit(solution)/shard_map/ppermute | solution.py:19
  28.9 27.0 %collective-permute-start.1 = (bf16[64,128,128]{2,1,0:T(8,128)(2,1)}, bf16[64,128,128]{2,1,0:T(8,128)(2,1)S(1)}, u32[]{:S(2)}, u32[]{:S(2)}) collective-permute-start(bf16[64,128,128]{2,1,0:T(8,128)(2,1)} %collective-permute-done.refs_1_), channel_id=1, source_target_pairs={{1,3},{3,5},{5,7},{9,11},{11,13},{13,15},{17,19},{19,21},{21,23},{... | collective-permute-start | bytes 6291464 | tf_op jit(solution)/shard_map/ppermute | solution.py:19
  30.2 25.7 %collective-permute-start.3 = (bf16[64,128,128]{2,1,0:T(8,128)(2,1)}, bf16[64,128,128]{2,1,0:T(8,128)(2,1)}, u32[]{:S(2)}, u32[]{:S(2)}) collective-permute-start(bf16[64,128,128]{2,1,0:T(8,128)(2,1)} %collective-permute-done.2.refs_0_), channel_id=1, source_target_pairs={{3,1},{11,9},{19,17},{27,25},{35,33},{43,41},{51,49},{59,57},{67,6... | collective-permute-start | bytes 6291464 | tf_op jit(solution)/shard_map/ppermute | solution.py:19
  32.2 29.0 %collective-permute-start.5 = (bf16[64,128,128]{2,1,0:T(8,128)(2,1)}, bf16[64,128,128]{2,1,0:T(8,128)(2,1)}, u32[]{:S(2)}, u32[]{:S(2)}) collective-permute-start(bf16[64,128,128]{2,1,0:T(8,128)(2,1)} %collective-permute-done.4), channel_id=1, source_target_pairs={{14,7},{22,15},{30,23},{38,31},{46,39},{54,47},{62,55},{70,63},{78... | collective-permute-start | bytes 6291464 | tf_op jit(solution)/shard_map/ppermute | solution.py:19
  33.5 1.6 %copy-start = (bf16[2,32,128,128]{3,2,1,0:T(8,128)(2,1)S(1)}, bf16[2,32,128,128]{3,2,1,0:T(8,128)(2,1)}, u32[]{:S(2)}) copy-start(bf16[2,32,128,128]{3,2,1,0:T(8,128)(2,1)} %param.2) | copy-start | bytes 6291460
  35.1 0.7 copy-start.1
  71.2 37.7 %collective-permute-start.6 = (bf16[2,16,128,128]{3,2,1,0:T(8,128)(2,1)S(1)}, bf16[2,16,128,128]{3,2,1,0:T(8,128)(2,1)S(1)}, u32[]{:S(2)}, u32[]{:S(2)}) collective-permute-start(bf16[2,16,128,128]{3,2,1,0:T(8,128)(2,1)S(1)} %get-tuple-element.8), channel_id=1, source_target_pairs={{1,0},{3,2},{5,4},{7,6},{9,8},{11,10},{13,12},{15,14},{17,16},{19,... | collective-permute-start | bytes 3145736 | tf_op jit(solution)/shard_map/ppermute | solution.py:19

commit v2 on v1

v2 whole, which is shorter than its diff:
```python
import functools

import jax
import jax.numpy as jnp
from jax import lax
from jax.experimental import pallas as pl
from jax.experimental.pallas import tpu as pltpu
from jax.sharding import PartitionSpec as P


UNROLL = 8
SENDER = 0
WORKER = 1


def move(value, routes):
    layers = lax.axis_size("depth")
    pairs = [(a * layers + b, c * layers + d) for (a, b), (c, d) in routes]
    return lax.ppermute(value, ("blk", "depth"), pairs)


def groups_here(tasks):
    column = lax.axis_index("blk") % tasks.shape[1]
    works = lax.axis_index("depth") == WORKER
    groups = jnp.where(works, tasks.shape[2] // UNROLL, 0)
    first, final = column == 0, column == tasks.shape[1] - 1
    return groups, first, final


def run_tasks(tasks, offset, groups, mine, panel, total):
    def group(step, carry):
        base = step * UNROLL
        products = []
        for n in range(UNROLL):
            first = mine[tasks[0, offset, base + n]]
            second = panel[tasks[1, offset, base + n]]
            products.append(jnp.dot(first, second, preferred_element_type=jnp.float32))
        for n in range(UNROLL):
            slot = tasks[2, offset, base + n]
            total[slot] = total[slot] + products[n]
        return carry

    lax.fori_loop(0, groups, group, 0)


def begin_kernel(tasks, mine, total):
    def clear(slot, carry):
        total[slot] = jnp.zeros(total.shape[1:], total.dtype)
        return carry

    works = lax.axis_index("depth") == WORKER
    lax.fori_loop(0, jnp.where(works, total.shape[0], 0), clear, 0)


def load(tasks, plan, arrived):
    copy = pltpu.make_async_copy(tasks, plan, arrived)
    copy.start()
    copy.wait()


def early_kernel(tasks, mine, one, three, before, total, plan, arrived):
    groups, _, final = groups_here(plan)

    @pl.when(groups > 0)
    def _():
        load(tasks, plan, arrived)
        run_tasks(plan, 0, groups, mine, mine, total)
        run_tasks(plan, 1, jnp.where(final, 0, groups), mine, one, total)
        run_tasks(plan, 3, groups, mine, three, total)


def relay_kernel(tasks, mine, up, down, before, total, plan, arrived):
    groups, first, _ = groups_here(plan)

    @pl.when(groups > 0)
    def _():
        load(tasks, plan, arrived)
        run_tasks(plan, 2, jnp.where(first, 0, groups), mine, up, total)
        run_tasks(plan, 2, jnp.where(first, groups, 0), mine, down, total)


def late_kernel(tasks, mine, crossed, total, low, high, plan, arrived):
    groups, _, final = groups_here(plan)

    @pl.when(final & (groups > 0))
    def _():
        load(tasks, plan, arrived)
        run_tasks(plan, 1, groups, mine, crossed, total)

    rows, half = low.shape[0], low.shape[1]
    for row in range(rows):

        def put(slot, carry):
            low[row, slot] = total[row * 2 * half + slot].astype(low.dtype)
            high[row, slot] = total[row * 2 * half + half + slot].astype(high.dtype)
            return carry

        lax.fori_loop(0, jnp.where(groups > 0, half, 0), put, 0)


def finish_kernel(high, sent, result, arrived):
    works = lax.axis_index("depth") == WORKER
    for used, source in ((works, high), (~works, sent)):

        @pl.when(used)
        def _():
            copy = pltpu.make_async_copy(source, result, arrived)
            copy.start()
            copy.wait()


VMEM = functools.partial(pl.BlockSpec, memory_space=pltpu.VMEM)
HBM = functools.partial(pl.BlockSpec, memory_space=pltpu.HBM)


def granted(mib):
    return pltpu.CompilerParams(vmem_limit_bytes=int(mib * 1024 * 1024))


def cost(blocks, size, tasks):
    return pl.CostEstimate(
        flops=2 * tasks * size**3, bytes_accessed=blocks * size * size * 2, transcendentals=0
    )


def body(density, product_tasks):
    rows, slots, size = density.shape[0], density.shape[1], density.shape[2]
    mine = density.reshape(rows * slots, size, size)
    tasks = product_tasks[:, 0]
    window, places = tasks.shape[1], tasks.shape[2]
    count = lax.axis_size("blk")
    lines = range(count // window)

    def at(line, column):
        return line % len(lines) * window + column

    inner = range(1, window)
    near = [((at(z, x), WORKER), (at(z, x - 1), WORKER)) for z in lines for x in inner]
    far = [((at(z, window - 1), WORKER), (at(z, 0), WORKER)) for z in lines]
    far += [((at(z + 1, x - 1), SENDER), (at(z, x), WORKER)) for z in lines for x in inner]
    ahead = [((at(z, 0), WORKER), (at(z, window - 1), SENDER)) for z in lines]
    across = [((at(z + 1, window - 1), SENDER), (at(z, window - 1), WORKER)) for z in lines]
    up = [((at(z, x - 1), WORKER), (at(z, x), WORKER)) for z in lines for x in inner]
    down = [((at(z, 1), WORKER), (at(z, 0), WORKER)) for z in lines]
    halves = [((p, WORKER), (p, SENDER)) for p in range(count)]

    moved = move(mine, ahead)
    one = move(mine, near)
    three = move(mine, far)
    crossed = move(moved, across)
    two_up = move(three, up)
    two_down = move(one, down)

    sums = jax.ShapeDtypeStruct((rows * slots + 1, size, size), jnp.float32)
    half = jax.ShapeDtypeStruct((rows, slots // 2, size, size), jnp.bfloat16)
    scratch = [pltpu.SMEM(tasks.shape, tasks.dtype), pltpu.SemaphoreType.DMA]
    total = pl.pallas_call(
        begin_kernel,
        out_shape=sums,
        in_specs=[HBM(), VMEM()],
        out_specs=VMEM(),
        compiler_params=granted(14),
        name="begin",
    )(tasks, mine)
    total = pl.pallas_call(
        early_kernel,
        out_shape=sums,
        in_specs=[HBM()] + [VMEM()] * 4,
        out_specs=VMEM(),
        input_output_aliases={4: 0},
        scratch_shapes=scratch,
        cost_estimate=cost(3 * slots, size, 3 * places),
        compiler_params=granted(14),
        name="early",
    )(tasks, mine, one, three, total)
    total = pl.pallas_call(
        relay_kernel,
        out_shape=sums,
        in_specs=[HBM()] + [VMEM()] * 4,
        out_specs=VMEM(),
        input_output_aliases={4: 0},
        scratch_shapes=scratch,
        cost_estimate=cost(3 * slots, size, places),
        compiler_params=granted(14),
        name="relay",
    )(tasks, mine, two_up, two_down, total)
    low, high = pl.pallas_call(
        late_kernel,
        out_shape=(half, half),
        in_specs=[HBM()] + [VMEM()] * 3,
        out_specs=(VMEM(), VMEM()),
        scratch_shapes=scratch,
        cost_estimate=cost(2 * slots, size, places),
        compiler_params=granted(14),
        name="late",
    )(tasks, mine, crossed, total)
    arrived = move(low, halves)
    return pl.pallas_call(
        finish_kernel,
        out_shape=half,
        in_specs=[VMEM(), HBM()],
        out_specs=HBM(),
        scratch_shapes=[pltpu.SemaphoreType.DMA],
        compiler_params=granted(14),
        name="finish",
    )(high, arrived)


def solution(mesh):
    placed = (P(("shift", "blk"), None, None, None), P(None, ("shift", "blk"), None, None))
    return jax.shard_map(
        body,
        mesh=mesh,
        in_specs=placed,
        out_specs=P(("shift", "blk"), "depth", None, None),
        check_vma=False,
    )
```

time: 110 us -> 106 us (0.964)
  Pallas kernels: 20.7 us -> 18.3 us
  other arithmetic: 1.24 us -> 0 us
    pallas_call x3 -> x5, Pallas kernels: 20.7 us -> 18.3 us  [the longest x1 8 us: body(): pl.pallas_call(early_kernel, out_shape=sums, in_specs=[HBM()] + [VMEM()]...]
  transfers between devices with their start and end apart: 7 -> 7, of which waited for: 4 -> 3; matrix products, arithmetic and copies ran while one was open for 0% -> 0% of each run, Pallas kernels for 10% -> 12%
where the time goes in v2:
time: 106 us
  starting transfers between devices  46.2 us (44%)
  waiting for transfers between devices  39.1 us (37%)
  Pallas kernels  18.3 us (17%)
  local copies, waits for them, and re-layouts  2.28 us (2%)
    ppermute x7, starting transfers between devices, move(): return lax.ppermute(value, ('blk', 'depth'), pairs)  46.2 us
    ppermute x7, waiting for transfers between devices, move(): return lax.ppermute(value, ('blk', 'depth'), pairs)  39.1 us
    pallas_call x1, Pallas kernels, body(): pl.pallas_call(early_kernel, out_shape=sums, in_specs=[HBM()] + [VMEM()]...  8 us
    pallas_call x1, Pallas kernels, body(): pl.pallas_call(late_kernel, out_shape=(half, half), in_specs=[HBM()] + [V...  4.64 us
    pallas_call x1, Pallas kernels, body(): pl.pallas_call(relay_kernel, out_shape=sums, in_specs=[HBM()] + [VMEM()]...  4.32 us
    unnamed x4, local copies, waits for them, and re-layouts  2.28 us
  transfers between devices with their start and end apart: 7, of which 3 were waited for; matrix products, arithmetic and copies ran while one was open for 0% of the time, Pallas kernels for 12%

profile of v2, /device:TPU:39, one launch (start us, length us, event | category | flops | bytes accessed | tf_op | source)
XLA Modules:
  0.0 106.0 jit_solution(15169732240245756930)
XLA Ops:
  0.0 1.9 %collective-permute-start.2 = (bf16[64,128,128]{2,1,0:T(8,128)(2,1)}, bf16[64,128,128]{2,1,0:T(8,128)(2,1)S(1)}, u32[]{:S(2)}, u32[]{:S(2)}) collective-permute-start(bf16[64,128,128]{2,1,0:T(8,128)(2,1)} %bitcast.2), channel_id=1, source_target_pairs={{7,1},{15,9},{23,17},{31,25},{39,33},{47,41},{55,49},{63,57},{71,6... | collective-permute-start | bytes 6291464 | tf_op jit(solution)/shard_map/ppermute | solution.py:19
  1.9 1.8 %collective-permute-start.4 = (bf16[64,128,128]{2,1,0:T(8,128)(2,1)}, bf16[64,128,128]{2,1,0:T(8,128)(2,1)S(1)}, u32[]{:S(2)}, u32[]{:S(2)}) collective-permute-start(bf16[64,128,128]{2,1,0:T(8,128)(2,1)} %bitcast.3), channel_id=1, source_target_pairs={{3,1},{5,3},{7,5},{11,9},{13,11},{15,13},{19,17},{21,19},{23,21},{... | collective-permute-start | bytes 6291464 | tf_op jit(solution)/shard_map/ppermute | solution.py:19
  3.8 0.8 collective-permute-start
  4.6 24.2 %collective-permute-done.2.three = bf16[64,128,128]{2,1,0:T(8,128)(2,1)S(1)} collective-permute-done((bf16[64,128,128]{2,1,0:T(8,128)(2,1)}, bf16[64,128,128]{2,1,0:T(8,128)(2,1)S(1)}, u32[]{:S(2)}, u32[]{:S(2)}) %collective-permute-start.2) | collective-permute-done | bytes 2097184 | tf_op jit(solution)/shard_map/ppermute | solution.py:19
  28.8 1.3 %collective-permute-start.3 = (bf16[64,128,128]{2,1,0:T(8,128)(2,1)S(1)}, bf16[64,128,128]{2,1,0:T(8,128)(2,1)S(1)}, u32[]{:S(2)}, u32[]{:S(2)}) collective-permute-start(bf16[64,128,128]{2,1,0:T(8,128)(2,1)S(1)} %collective-permute-done.2.three), channel_id=1, source_target_pairs={{1,3},{3,5},{5,7},{9,11},{11,13},{13,15},{17,19},{19,21},{21,23},{... | collective-permute-start | bytes 6291464 | tf_op jit(solution)/shard_map/ppermute | solution.py:19
  30.1 0.0 collective-permute-done.4.one
  30.1 0.8 collective-permute-start.5
  30.9 0.0 collective-permute-done
  30.9 1.3 %collective-permute-start.1 = (bf16[64,128,128]{2,1,0:T(8,128)(2,1)S(1)}, bf16[64,128,128]{2,1,0:T(8,128)(2,1)S(1)}, u32[]{:S(2)}, u32[]{:S(2)}) collective-permute-start(bf16[64,128,128]{2,1,0:T(8,128)(2,1)S(1)} %collective-permute-done), channel_id=1, source_target_pairs={{14,7},{22,15},{30,23},{38,31},{46,39},{54,47},{62,55},{70,63},{78... | collective-permute-start | bytes 6291464 | tf_op jit(solution)/shard_map/ppermute | solution.py:19
  32.2 0.0 copy-start
  32.2 1.6 %copy-done = bf16[2,32,128,128]{3,2,1,0:T(8,128)(2,1)S(1)} copy-done((bf16[2,32,128,128]{3,2,1,0:T(8,128)(2,1)S(1)}, bf16[2,32,128,128]{3,2,1,0:T(8,128)(2,1)}, u32[]{:S(2)}) %copy-start) | copy-done | bytes 2097176
  33.8 0.0 copy-start.1
  33.8 0.7 copy-done.1
  34.5 0.3 begin.1.before
  34.9 8.0 %early.1.before = f32[65,128,128]{2,1,0:T(8,128)S(1)} custom-call(s32[3,4,128]{2,1,0:T(4,128)S(1)} %bitcast.10, bf16[64,128,128]{2,1,0:T(8,128)(2,1)S(1)} %bitcast.6, bf16[64,128,128]{2,1,0:T(8,128)(2,1)S(1)} %collective-permute-done.4.one, bf16[64,128,128]{2,1,0:T(8,128)(2,1)S(1)} %collective-permute-done.2.three, ...), custom_call_target="tpu_custom_call", output_to_operand_aliasing={{}: (4, {})} | custom-call | flops 1610612736 | bytes 3145728 | tf_op jit(solution)/shard_map/early/pallas_call | solution.py:165
  42.9 12.7 %collective-permute-done.3.up = bf16[64,128,128]{2,1,0:T(8,128)(2,1)S(1)} collective-permute-done((bf16[64,128,128]{2,1,0:T(8,128)(2,1)S(1)}, bf16[64,128,128]{2,1,0:T(8,128)(2,1)S(1)}, u32[]{:S(2)}, u32[]{:S(2)}) %collective-permute-start.3) | collective-permute-done | bytes 2097184 | tf_op jit(solution)/shard_map/ppermute | solution.py:19
  55.6 0.0 collective-permute-done.5.down
  55.6 4.3 %relay.1.total = f32[65,128,128]{2,1,0:T(8,128)S(1)} custom-call(s32[3,4,128]{2,1,0:T(4,128)S(1)} %bitcast.11, bf16[64,128,128]{2,1,0:T(8,128)(2,1)S(1)} %bitcast.7, bf16[64,128,128]{2,1,0:T(8,128)(2,1)S(1)} %collective-permute-done.3.up, bf16[64,128,128]{2,1,0:T(8,128)(2,1)S(1)} %collective-permute-done.5.down, ...), custom_call_target="tpu_custom_call", output_to_operand_aliasing={{}: (4, {})} | custom-call | flops 536870912 | bytes 3145728 | tf_op jit(solution)/shard_map/relay/pallas_call | solution.py:176
  59.9 0.0 collective-permute-done.1.crossed
  59.9 4.6 %late.1 = (bf16[2,16,128,128]{3,2,1,0:T(8,128)(2,1)S(1)}, bf16[2,16,128,128]{3,2,1,0:T(8,128)(2,1)S(1)}) custom-call(s32[3,4,128]{2,1,0:T(4,128)S(1)} %bitcast.12, bf16[64,128,128]{2,1,0:T(8,128)(2,1)S(1)} %bitcast.8, bf16[64,128,128]{2,1,0:T(8,128)(2,1)S(1)} %collective-permute-done.1.crossed, f32[65,128,128]{2,1,0:T(8,128)S(1)} %relay.1.total), custom_call_target="tpu_custom_call" | custom-call | flops 536870912 | bytes 2097152 | tf_op jit(solution)/shard_map/late/pallas_call | solution.py:187
  64.6 38.3 %collective-permute-start.6 = (bf16[2,16,128,128]{3,2,1,0:T(8,128)(2,1)S(1)}, bf16[2,16,128,128]{3,2,1,0:T(8,128)(2,1)S(1)}, u32[]{:S(2)}, u32[]{:S(2)}) collective-permute-start(bf16[2,16,128,128]{3,2,1,0:T(8,128)(2,1)S(1)} %get-tuple-element.8), channel_id=1, source_target_pairs={{1,0},{3,2},{5,4},{7,6},{9,8},{11,10},{13,12},{15,14},{17,16},{19,... | collective-permute-start | bytes 3145736 | tf_op jit(solution)/shard_map/ppermute | solution.py:19
  102.8 2.2 %collective-permute-done.6.sent = bf16[2,16,128,128]{3,2,1,0:T(8,128)(2,1)S(1)} collective-permute-done((bf16[2,16,128,128]{3,2,1,0:T(8,128)(2,1)S(1)}, bf16[2,16,128,128]{3,2,1,0:T(8,128)(2,1)S(1)}, u32[]{:S(2)}, u32[]{:S(2)}) %collective-permute-start.6) | collective-permute-done | bytes 1048608 | tf_op jit(solution)/shard_map/ppermute | solution.py:19
  105.0 1.0 finish.1
Async XLA Ops:
  0.0 28.8 %collective-permute-start.2 = (bf16[64,128,128]{2,1,0:T(8,128)(2,1)}, bf16[64,128,128]{2,1,0:T(8,128)(2,1)S(1)}, u32[]{:S(2)}, u32[]{:S(2)}) collective-permute-start(bf16[64,128,128]{2,1,0:T(8,128)(2,1)} %bitcast.2), channel_id=1, source_target_pairs={{7,1},{15,9},{23,17},{31,25},{39,33},{47,41},{55,49},{63,57},{71,6... | collective-permute-start | bytes 6291464 | tf_op jit(solution)/shard_map/ppermute | solution.py:19
  1.9 28.1 %collective-permute-start.4 = (bf16[64,128,128]{2,1,0:T(8,128)(2,1)}, bf16[64,128,128]{2,1,0:T(8,128)(2,1)S(1)}, u32[]{:S(2)}, u32[]{:S(2)}) collective-permute-start(bf16[64,128,128]{2,1,0:T(8,128)(2,1)} %bitcast.3), channel_id=1, source_target_pairs={{3,1},{5,3},{7,5},{11,9},{13,11},{15,13},{19,17},{21,19},{23,21},{... | collective-permute-start | bytes 6291464 | tf_op jit(solution)/shard_map/ppermute | solution.py:19
  3.8 27.1 %collective-permute-start = (bf16[64,128,128]{2,1,0:T(8,128)(2,1)}, bf16[64,128,128]{2,1,0:T(8,128)(2,1)S(1)}, u32[]{:S(2)}, u32[]{:S(2)}) collective-permute-start(bf16[64,128,128]{2,1,0:T(8,128)(2,1)} %bitcast.4), channel_id=1, source_target_pairs={{1,6},{9,14},{17,22},{25,30},{33,38},{41,46},{49,54},{57,62},{65,7... | collective-permute-start | bytes 6291464 | tf_op jit(solution)/shard_map/ppermute | solution.py:19
  28.8 26.8 %collective-permute-start.3 = (bf16[64,128,128]{2,1,0:T(8,128)(2,1)S(1)}, bf16[64,128,128]{2,1,0:T(8,128)(2,1)S(1)}, u32[]{:S(2)}, u32[]{:S(2)}) collective-permute-start(bf16[64,128,128]{2,1,0:T(8,128)(2,1)S(1)} %collective-permute-done.2.three), channel_id=1, source_target_pairs={{1,3},{3,5},{5,7},{9,11},{11,13},{13,15},{17,19},{19,21},{21,23},{... | collective-permute-start | bytes 6291464 | tf_op jit(solution)/shard_map/ppermute | solution.py:19
  30.1 25.5 %collective-permute-start.5 = (bf16[64,128,128]{2,1,0:T(8,128)(2,1)S(1)}, bf16[64,128,128]{2,1,0:T(8,128)(2,1)S(1)}, u32[]{:S(2)}, u32[]{:S(2)}) collective-permute-start(bf16[64,128,128]{2,1,0:T(8,128)(2,1)S(1)} %collective-permute-done.4.one), channel_id=1, source_target_pairs={{3,1},{11,9},{19,17},{27,25},{35,33},{43,41},{51,49},{59,57},{67,6... | collective-permute-start | bytes 6291464 | tf_op jit(solution)/shard_map/ppermute | solution.py:19
  30.9 29.0 %collective-permute-start.1 = (bf16[64,128,128]{2,1,0:T(8,128)(2,1)S(1)}, bf16[64,128,128]{2,1,0:T(8,128)(2,1)S(1)}, u32[]{:S(2)}, u32[]{:S(2)}) collective-permute-start(bf16[64,128,128]{2,1,0:T(8,128)(2,1)S(1)} %collective-permute-done), channel_id=1, source_target_pairs={{14,7},{22,15},{30,23},{38,31},{46,39},{54,47},{62,55},{70,63},{78... | collective-permute-start | bytes 6291464 | tf_op jit(solution)/shard_map/ppermute | solution.py:19
  32.2 1.6 %copy-start = (bf16[2,32,128,128]{3,2,1,0:T(8,128)(2,1)S(1)}, bf16[2,32,128,128]{3,2,1,0:T(8,128)(2,1)}, u32[]{:S(2)}) copy-start(bf16[2,32,128,128]{3,2,1,0:T(8,128)(2,1)} %param.2) | copy-start | bytes 6291460
  33.8 0.7 copy-start.1
  64.6 40.5 %collective-permute-start.6 = (bf16[2,16,128,128]{3,2,1,0:T(8,128)(2,1)S(1)}, bf16[2,16,128,128]{3,2,1,0:T(8,128)(2,1)S(1)}, u32[]{:S(2)}, u32[]{:S(2)}) collective-permute-start(bf16[2,16,128,128]{3,2,1,0:T(8,128)(2,1)S(1)} %get-tuple-element.8), channel_id=1, source_target_pairs={{1,0},{3,2},{5,4},{7,6},{9,8},{11,10},{13,12},{15,14},{17,16},{19,... | collective-permute-start | bytes 3145736 | tf_op jit(solution)/shard_map/ppermute | solution.py:19

commit v3 on v2

--- a/solution.py
+++ b/solution.py
@@ -98,15 +98,14 @@
         lax.fori_loop(0, jnp.where(groups > 0, half, 0), put, 0)
 
 
-def finish_kernel(high, sent, result, arrived):
-    works = lax.axis_index("depth") == WORKER
-    for used, source in ((works, high), (~works, sent)):
-
-        @pl.when(used)
-        def _():
-            copy = pltpu.make_async_copy(source, result, arrived)
-            copy.start()
-            copy.wait()
+def write_kernel(used_by, source, *refs):
+    result, arrived = refs[-2:]
+
+    @pl.when(lax.axis_index("depth") == used_by)
+    def _():
+        copy = pltpu.make_async_copy(source, result, arrived)
+        copy.start()
+        copy.wait()
 
 
 VMEM = functools.partial(pl.BlockSpec, memory_space=pltpu.VMEM)
@@ -135,8 +134,9 @@
         return line % len(lines) * window + column
 
     inner = range(1, window)
-    near = [((at(z, x), WORKER), (at(z, x - 1), WORKER)) for z in lines for x in inner]
-    far = [((at(z, window - 1), WORKER), (at(z, 0), WORKER)) for z in lines]
+    starts = [WORKER] * (window - 1) + [SENDER]
+    near = [((at(z, x), starts[x]), (at(z, x - 1), WORKER)) for z in lines for x in inner]
+    far = [((at(z, window - 1), SENDER), (at(z, 0), WORKER)) for z in lines]
     far += [((at(z + 1, x - 1), SENDER), (at(z, x), WORKER)) for z in lines for x in inner]
     ahead = [((at(z, 0), WORKER), (at(z, window - 1), SENDER)) for z in lines]
     across = [((at(z + 1, window - 1), SENDER), (at(z, window - 1), WORKER)) for z in lines]
@@ -194,16 +194,26 @@
         compiler_params=granted(14),
         name="late",
     )(tasks, mine, crossed, total)
-    arrived = move(low, halves)
+    result = pl.pallas_call(
+        functools.partial(write_kernel, WORKER),
+        out_shape=half,
+        in_specs=[VMEM()],
+        out_specs=HBM(),
+        scratch_shapes=[pltpu.SemaphoreType.DMA],
+        compiler_params=granted(14),
+        name="own",
+    )(high)
+    sent = move(low, halves)
     return pl.pallas_call(
-        finish_kernel,
+        functools.partial(write_kernel, SENDER),
         out_shape=half,
         in_specs=[VMEM(), HBM()],
         out_specs=HBM(),
+        input_output_aliases={1: 0},
         scratch_shapes=[pltpu.SemaphoreType.DMA],
         compiler_params=granted(14),
-        name="finish",
-    )(high, arrived)
+        name="other",
+    )(sent, result)
 
 
 def solution(mesh):

time: 106 us -> 106 us (level)
  the two profiles are of different devices: /device:TPU:39 before, /device:TPU:38 now
where the time goes in v3:
time: 106 us
  starting transfers between devices  52.2 us (49%)
  waiting for transfers between devices  50.2 us (47%)
  local copies, waits for them, and re-layouts  2.28 us (2%)
    ppermute x7, starting transfers between devices, move(): return lax.ppermute(value, ('blk', 'depth'), pairs)  52.2 us
    ppermute x7, waiting for transfers between devices, move(): return lax.ppermute(value, ('blk', 'depth'), pairs)  50.2 us
    unnamed x4, local copies, waits for them, and re-layouts  2.28 us
  transfers between devices with their start and end apart: 7, of which 5 were waited for; matrix products, arithmetic and copies ran while one was open for 0% of the time, Pallas kernels for 0%

profile of v3, /device:TPU:38, one launch (start us, length us, event | category | flops | bytes accessed | tf_op | source)
XLA Modules:
  0.0 105.8 jit_solution(1076100942597422681)
XLA Ops:
  0.0 1.4 %collective-permute-start.2 = (bf16[64,128,128]{2,1,0:T(8,128)(2,1)}, bf16[64,128,128]{2,1,0:T(8,128)(2,1)S(1)}, u32[]{:S(2)}, u32[]{:S(2)}) collective-permute-start(bf16[64,128,128]{2,1,0:T(8,128)(2,1)} %bitcast.2), channel_id=1, source_target_pairs={{6,1},{14,9},{22,17},{30,25},{38,33},{46,41},{54,49},{62,57},{70,6... | collective-permute-start | bytes 6291464 | tf_op jit(solution)/shard_map/ppermute | solution.py:19
  1.4 2.1 %collective-permute-start.4 = (bf16[64,128,128]{2,1,0:T(8,128)(2,1)}, bf16[64,128,128]{2,1,0:T(8,128)(2,1)S(1)}, u32[]{:S(2)}, u32[]{:S(2)}) collective-permute-start(bf16[64,128,128]{2,1,0:T(8,128)(2,1)} %bitcast.3), channel_id=1, source_target_pairs={{3,1},{5,3},{6,5},{11,9},{13,11},{14,13},{19,17},{21,19},{22,21},{... | collective-permute-start | bytes 6291464 | tf_op jit(solution)/shard_map/ppermute | solution.py:19
  3.6 1.3 %collective-permute-start = (bf16[64,128,128]{2,1,0:T(8,128)(2,1)}, bf16[64,128,128]{2,1,0:T(8,128)(2,1)S(1)}, u32[]{:S(2)}, u32[]{:S(2)}) collective-permute-start(bf16[64,128,128]{2,1,0:T(8,128)(2,1)} %bitcast.4), channel_id=1, source_target_pairs={{1,6},{9,14},{17,22},{25,30},{33,38},{41,46},{49,54},{57,62},{65,7... | collective-permute-start | bytes 6291464 | tf_op jit(solution)/shard_map/ppermute | solution.py:19
  4.9 20.3 %collective-permute-done.2.three = bf16[64,128,128]{2,1,0:T(8,128)(2,1)S(1)} collective-permute-done((bf16[64,128,128]{2,1,0:T(8,128)(2,1)}, bf16[64,128,128]{2,1,0:T(8,128)(2,1)S(1)}, u32[]{:S(2)}, u32[]{:S(2)}) %collective-permute-start.2) | collective-permute-done | bytes 2097184 | tf_op jit(solution)/shard_map/ppermute | solution.py:19
  25.2 0.8 collective-permute-start.3
  25.9 1.4 %collective-permute-done.4.one = bf16[64,128,128]{2,1,0:T(8,128)(2,1)S(1)} collective-permute-done((bf16[64,128,128]{2,1,0:T(8,128)(2,1)}, bf16[64,128,128]{2,1,0:T(8,128)(2,1)S(1)}, u32[]{:S(2)}, u32[]{:S(2)}) %collective-permute-start.4) | collective-permute-done | bytes 2097184 | tf_op jit(solution)/shard_map/ppermute | solution.py:19
  27.3 0.8 collective-permute-start.5
  28.1 4.3 %collective-permute-done = bf16[64,128,128]{2,1,0:T(8,128)(2,1)S(1)} collective-permute-done((bf16[64,128,128]{2,1,0:T(8,128)(2,1)}, bf16[64,128,128]{2,1,0:T(8,128)(2,1)S(1)}, u32[]{:S(2)}, u32[]{:S(2)}) %collective-permute-start) | collective-permute-done | bytes 2097184 | tf_op jit(solution)/shard_map/ppermute | solution.py:19
  32.4 44.4 %collective-permute-start.1 = (bf16[64,128,128]{2,1,0:T(8,128)(2,1)S(1)}, bf16[64,128,128]{2,1,0:T(8,128)(2,1)S(1)}, u32[]{:S(2)}, u32[]{:S(2)}) collective-permute-start(bf16[64,128,128]{2,1,0:T(8,128)(2,1)S(1)} %collective-permute-done), channel_id=1, source_target_pairs={{14,7},{22,15},{30,23},{38,31},{46,39},{54,47},{62,55},{70,63},{78... | collective-permute-start | bytes 6291464 | tf_op jit(solution)/shard_map/ppermute | solution.py:19
  76.8 0.0 copy-start
  76.8 1.6 %copy-done = bf16[2,32,128,128]{3,2,1,0:T(8,128)(2,1)S(1)} copy-done((bf16[2,32,128,128]{3,2,1,0:T(8,128)(2,1)S(1)}, bf16[2,32,128,128]{3,2,1,0:T(8,128)(2,1)}, u32[]{:S(2)}) %copy-start) | copy-done | bytes 2097176
  78.4 0.0 copy-start.1
  78.4 0.7 copy-done.1
  79.1 0.0 collective-permute-done.3.up
  79.1 0.0 collective-permute-done.5.down
  79.2 21.0 %collective-permute-done.1.crossed = bf16[64,128,128]{2,1,0:T(8,128)(2,1)S(1)} collective-permute-done((bf16[64,128,128]{2,1,0:T(8,128)(2,1)S(1)}, bf16[64,128,128]{2,1,0:T(8,128)(2,1)S(1)}, u32[]{:S(2)}, u32[]{:S(2)}) %collective-permute-start.1) | collective-permute-done | bytes 2097184 | tf_op jit(solution)/shard_map/ppermute | solution.py:19
  100.2 1.3 %collective-permute-start.6 = (bf16[2,16,128,128]{3,2,1,0:T(8,128)(2,1)S(1)}, bf16[2,16,128,128]{3,2,1,0:T(8,128)(2,1)S(1)}, u32[]{:S(2)}, u32[]{:S(2)}) collective-permute-start(bf16[2,16,128,128]{3,2,1,0:T(8,128)(2,1)S(1)} %get-tuple-element.7), channel_id=1, source_target_pairs={{1,0},{3,2},{5,4},{7,6},{9,8},{11,10},{13,12},{15,14},{17,16},{19,... | collective-permute-start | bytes 3145736 | tf_op jit(solution)/shard_map/ppermute | solution.py:19
  101.6 3.2 %collective-permute-done.6.source = bf16[2,16,128,128]{3,2,1,0:T(8,128)(2,1)S(1)} collective-permute-done((bf16[2,16,128,128]{3,2,1,0:T(8,128)(2,1)S(1)}, bf16[2,16,128,128]{3,2,1,0:T(8,128)(2,1)S(1)}, u32[]{:S(2)}, u32[]{:S(2)}) %collective-permute-start.6) | collective-permute-done | bytes 1048608 | tf_op jit(solution)/shard_map/ppermute | solution.py:19
  104.8 1.0 other.1
  (5 shorter events, 0.1 us)
Async XLA Ops:
  0.0 25.2 %collective-permute-start.2 = (bf16[64,128,128]{2,1,0:T(8,128)(2,1)}, bf16[64,128,128]{2,1,0:T(8,128)(2,1)S(1)}, u32[]{:S(2)}, u32[]{:S(2)}) collective-permute-start(bf16[64,128,128]{2,1,0:T(8,128)(2,1)} %bitcast.2), channel_id=1, source_target_pairs={{6,1},{14,9},{22,17},{30,25},{38,33},{46,41},{54,49},{62,57},{70,6... | collective-permute-start | bytes 6291464 | tf_op jit(solution)/shard_map/ppermute | solution.py:19
  1.4 25.9 %collective-permute-start.4 = (bf16[64,128,128]{2,1,0:T(8,128)(2,1)}, bf16[64,128,128]{2,1,0:T(8,128)(2,1)S(1)}, u32[]{:S(2)}, u32[]{:S(2)}) collective-permute-start(bf16[64,128,128]{2,1,0:T(8,128)(2,1)} %bitcast.3), channel_id=1, source_target_pairs={{3,1},{5,3},{6,5},{11,9},{13,11},{14,13},{19,17},{21,19},{22,21},{... | collective-permute-start | bytes 6291464 | tf_op jit(solution)/shard_map/ppermute | solution.py:19
  3.6 28.8 %collective-permute-start = (bf16[64,128,128]{2,1,0:T(8,128)(2,1)}, bf16[64,128,128]{2,1,0:T(8,128)(2,1)S(1)}, u32[]{:S(2)}, u32[]{:S(2)}) collective-permute-start(bf16[64,128,128]{2,1,0:T(8,128)(2,1)} %bitcast.4), channel_id=1, source_target_pairs={{1,6},{9,14},{17,22},{25,30},{33,38},{41,46},{49,54},{57,62},{65,7... | collective-permute-start | bytes 6291464 | tf_op jit(solution)/shard_map/ppermute | solution.py:19
  25.2 54.0 %collective-permute-start.3 = (bf16[64,128,128]{2,1,0:T(8,128)(2,1)S(1)}, bf16[64,128,128]{2,1,0:T(8,128)(2,1)S(1)}, u32[]{:S(2)}, u32[]{:S(2)}) collective-permute-start(bf16[64,128,128]{2,1,0:T(8,128)(2,1)S(1)} %collective-permute-done.2.three), channel_id=1, source_target_pairs={{1,3},{3,5},{5,7},{9,11},{11,13},{13,15},{17,19},{19,21},{21,23},{... | collective-permute-start | bytes 6291464 | tf_op jit(solution)/shard_map/ppermute | solution.py:19
  27.3 51.8 %collective-permute-start.5 = (bf16[64,128,128]{2,1,0:T(8,128)(2,1)S(1)}, bf16[64,128,128]{2,1,0:T(8,128)(2,1)S(1)}, u32[]{:S(2)}, u32[]{:S(2)}) collective-permute-start(bf16[64,128,128]{2,1,0:T(8,128)(2,1)S(1)} %collective-permute-done.4.one), channel_id=1, source_target_pairs={{3,1},{11,9},{19,17},{27,25},{35,33},{43,41},{51,49},{59,57},{67,6... | collective-permute-start | bytes 6291464 | tf_op jit(solution)/shard_map/ppermute | solution.py:19
  32.4 67.8 %collective-permute-start.1 = (bf16[64,128,128]{2,1,0:T(8,128)(2,1)S(1)}, bf16[64,128,128]{2,1,0:T(8,128)(2,1)S(1)}, u32[]{:S(2)}, u32[]{:S(2)}) collective-permute-start(bf16[64,128,128]{2,1,0:T(8,128)(2,1)S(1)} %collective-permute-done), channel_id=1, source_target_pairs={{14,7},{22,15},{30,23},{38,31},{46,39},{54,47},{62,55},{70,63},{78... | collective-permute-start | bytes 6291464 | tf_op jit(solution)/shard_map/ppermute | solution.py:19
  76.8 1.6 %copy-start = (bf16[2,32,128,128]{3,2,1,0:T(8,128)(2,1)S(1)}, bf16[2,32,128,128]{3,2,1,0:T(8,128)(2,1)}, u32[]{:S(2)}) copy-start(bf16[2,32,128,128]{3,2,1,0:T(8,128)(2,1)} %param.2) | copy-start | bytes 6291460
  78.4 0.7 copy-start.1
  100.2 4.6 %collective-permute-start.6 = (bf16[2,16,128,128]{3,2,1,0:T(8,128)(2,1)S(1)}, bf16[2,16,128,128]{3,2,1,0:T(8,128)(2,1)S(1)}, u32[]{:S(2)}, u32[]{:S(2)}) collective-permute-start(bf16[2,16,128,128]{3,2,1,0:T(8,128)(2,1)S(1)} %get-tuple-element.7), channel_id=1, source_target_pairs={{1,0},{3,2},{5,4},{7,6},{9,8},{11,10},{13,12},{15,14},{17,16},{19,... | collective-permute-start | bytes 3145736 | tf_op jit(solution)/shard_map/ppermute | solution.py:19
